TPU v7x, 8 devices: a whole 2x2x1 slice. The times are simulated.
8 devices in a mesh: replica: 1 (over z), model: 8 (over y, x, core).
Axes of the slice: x: 2, y: 2, z: 1, core: 2. Of those that a mesh axis runs over, the one named last changes fastest.
Arguments:
- x: bfloat16 [512, 2048], P('replica')
- w_query: bfloat16 [2048, 2048], P(None, 'model')
- w_key: bfloat16 [2048, 256], replicated
- w_value: bfloat16 [2048, 256], replicated
- w_out: bfloat16 [2048, 2048], P('model')
- k_cache: bfloat16 [512, 1, 2048, 256], P('replica')
- v_cache: bfloat16 [512, 1, 2048, 256], P('replica')
- lengths: int32 [512], P('replica')
Outputs:
- output 1: bfloat16 [512, 2048], P('replica')
- output 2: bfloat16 [512, 1, 256], P('replica')
- output 3: bfloat16 [512, 1, 256], P('replica')
All inputs are finite; a program needn't handle non-finite values.
Results may differ from a plain program's by a relative error of at most 0.00406014.
Values are sent between devices in bfloat16 or wider.
A program may use at most 4.25 GiB of HBM per device.

v0:
```python
import jax
import jax.numpy as jnp
from jax import lax
from jax.experimental import pallas as pl
from jax.experimental.pallas import tpu as pltpu
from jax.sharding import PartitionSpec as P

BF = jnp.bfloat16
F32 = jnp.float32
HEADS = 8
HD = 256
LOCAL = 64
SHORT = 32
GROUP = 16
CHUNK = 256
MAXLEN = 2048
SLOTS = 6
AHEAD = 4
HALFW = 128
MIB = 2 ** 20
SCALE = HD ** -0.5
DIMS_T = (((1,), (1,)), ((), ()))


def coords():
    me = lax.axis_index("model")
    return me, me // 4, (me // 2) % 2, me % 2


def peer(rel):
    _, y, x, k = coords()
    dy, dx, dk = rel // 4, (rel // 2) % 2, rel % 2
    return (((y + dy) % 2) * 2 + (x + dx) % 2) * 2 + (k + dk) % 2


def span(index, size):
    return pl.ds(pl.multiple_of(index * size, size), size)


def entry_barrier(rels):
    barrier = pltpu.get_barrier_semaphore()
    for rel in rels:
        pl.semaphore_signal(barrier, inc=1, device_id={"model": peer(rel)}, device_id_type=pl.DeviceIdType.MESH)
    pl.semaphore_wait(barrier, len(rels))


def remote(src, dst, send_sem, recv_sem, rel):
    return pltpu.make_async_remote_copy(
        src_ref=src, dst_ref=dst, send_sem=send_sem, recv_sem=recv_sem,
        device_id={"model": peer(rel)}, device_id_type=pl.DeviceIdType.MESH)


RELS = (6, 7, 2, 3, 4, 5, 1)


def softmax_parts(s, s_new):
    m = jnp.maximum(jnp.max(s, axis=-1, keepdims=True), s_new)
    e = jnp.exp(s - m)
    e_new = jnp.exp(s_new - m)
    total = jnp.sum(e, axis=-1, keepdims=True) + e_new
    return e.astype(BF), e_new.astype(BF).astype(F32), total


def project_kernel(len_hbm, x_hbm, wq_hbm, wk_hbm, wv_hbm, wo_hbm, k_hbm, v_hbm, q_out, kn_out, vn_out, wx_out, wy_out, o_out, wd_out,
                   x_v, wq_v, wk_v, wv_v, wo_v, q_v, ks, vs, lens_v, len_ref, in_sem, own_sem, qs, qr, ws, wr):
    me, y, x, k = coords()
    mine = span(me, LOCAL)
    loads = [pltpu.make_async_copy(src, dst, in_sem.at[i]) for i, (src, dst) in enumerate((
        (wq_hbm, wq_v),
        (wo_hbm, wo_v),
        (wk_hbm, wk_v),
        (wv_hbm, wv_v),
        (k_hbm.at[mine, 0, pl.ds(0, SHORT), :], ks),
        (v_hbm.at[mine, 0, pl.ds(0, SHORT), :], vs),
        (len_hbm, len_ref),
    ))]
    loads[0].start()
    blocks = []
    for i, chip_rel in enumerate((6, 2, 4, 0)):
        rows = span(peer(chip_rel) // 2, 2 * LOCAL)
        blocks.append(pltpu.make_async_copy(x_hbm.at[rows, :], x_v.at[rows, :], in_sem.at[7 + i]))
        blocks[-1].start()
    loads[1].start()
    entry_barrier(RELS)
    loads[0].wait()
    q_copies, w_copies = [], []
    for i, chip_rel in enumerate((6, 2, 4, 0)):
        rows = span(peer(chip_rel) // 2, 2 * LOCAL)
        blocks[i].wait()
        q_v[rows, :] = jnp.dot(x_v[rows, :], wq_v[...], preferred_element_type=F32).astype(BF)
        for rel in (chip_rel, chip_rel + 1):
            if rel == 0:
                continue
            copy = remote(q_v.at[span(peer(rel), LOCAL), :], q_out.at[me], qs.at[rel], qr.at[rel], rel)
            copy.start()
            q_copies.append(copy)
    loads[1].wait()
    for i, (rel, out) in enumerate(((X, wx_out), (Y, wy_out))):
        w_copies.append(remote(wo_v.at[:, span(peer(rel) // 2, 2 * HD)], out, ws.at[i], wr.at[i], rel))
        w_copies[i].start()
    store = pltpu.make_async_copy(wo_v.at[:, span(peer(D) // 2, 2 * HD)], wd_out, own_sem)
    store.start()
    for load in loads[2:7]:
        load.start()
    q_out[me] = q_v[mine, :]

    def spread(i, carry):
        lens_v[pl.ds(i, 1), :] = jnp.full((1, 128), len_ref[me * LOCAL + i], jnp.int32)
        return carry

    loads[6].wait()
    lax.fori_loop(0, LOCAL, spread, 0)
    for load in loads[2:6]:
        load.wait()
    for part in range(2):
        rows = pl.ds(part * 256, 256)
        kn_out[rows, :] = jnp.dot(x_v[rows, :], wk_v[...], preferred_element_type=F32).astype(BF)
        vn_out[rows, :] = jnp.dot(x_v[rows, :], wv_v[...], preferred_element_type=F32).astype(BF)
    for copy in q_copies:
        copy.wait()

    width = GROUP * SHORT
    col = lax.broadcasted_iota(jnp.int32, (GROUP, width), 1)
    same = (col // SHORT) == lax.broadcasted_iota(jnp.int32, (GROUP, width), 0)
    slot_pos = col % SHORT

    def group(g, carry):
        seqs = span(g, GROUP)
        new = pl.ds(pl.multiple_of(me * LOCAL + g * GROUP, GROUP), GROUP)
        qg = q_out[:, seqs, :]
        s = lax.dot_general(qg.reshape(HEADS * GROUP, HD), ks[seqs].reshape(width, HD), DIMS_T, preferred_element_type=F32) * SCALE
        valid = same & (slot_pos < lens_v[seqs, 0:1])
        s = jnp.where(valid[None], s.reshape(HEADS, GROUP, width), -jnp.inf)
        s_new = jnp.sum(qg.astype(F32) * kn_out[new, :].astype(F32)[None], axis=-1, keepdims=True) * SCALE
        e, e_new, total = softmax_parts(s, s_new)
        num = jnp.dot(e.reshape(HEADS * GROUP, width), vs[seqs].reshape(width, HD), preferred_element_type=F32)
        num = num.reshape(HEADS, GROUP, HD) + e_new * vn_out[new, :].astype(F32)[None]
        o_out[:, seqs, :] = (num / total).astype(BF)
        return carry

    lax.fori_loop(0, LOCAL // GROUP, group, 0)
    for copy in w_copies + [store]:
        copy.wait()


def project(lengths, x, wq, wk, wv, wo, k_cache, v_cache):
    rows, depth = x.shape
    hbm_spec = pl.BlockSpec(memory_space=pltpu.HBM)
    vmem_spec = pl.BlockSpec(memory_space=pltpu.VMEM)
    return pl.pallas_call(
        project_kernel,
        out_shape=(
            jax.ShapeDtypeStruct((HEADS, LOCAL, HD), BF),
            jax.ShapeDtypeStruct((rows, HD), BF),
            jax.ShapeDtypeStruct((rows, HD), BF),
            jax.ShapeDtypeStruct((HD, 2 * HD), BF),
            jax.ShapeDtypeStruct((HD, 2 * HD), BF),
            jax.ShapeDtypeStruct((HEADS, LOCAL, HD), BF),
            jax.ShapeDtypeStruct((HD, 2 * HD), BF),
        ),
        in_specs=[hbm_spec] * 8,
        out_specs=(vmem_spec,) * 6 + (hbm_spec,),
        scratch_shapes=[
            pltpu.VMEM((rows, depth), BF),
            pltpu.VMEM((depth, HD), BF),
            pltpu.VMEM((depth, HD), BF),
            pltpu.VMEM((depth, HD), BF),
            pltpu.VMEM(wo.shape, BF),
            pltpu.VMEM((rows, HD), BF),
            pltpu.VMEM((LOCAL, SHORT, HD), BF),
            pltpu.VMEM((LOCAL, SHORT, HD), BF),
            pltpu.VMEM((LOCAL, 128), jnp.int32),
            pltpu.SMEM(lengths.shape, jnp.int32),
            pltpu.SemaphoreType.DMA((11,)),
            pltpu.SemaphoreType.DMA,
            pltpu.SemaphoreType.DMA((8,)),
            pltpu.SemaphoreType.DMA((8,)),
            pltpu.SemaphoreType.DMA((2,)),
            pltpu.SemaphoreType.DMA((2,)),
        ],
        compiler_params=pltpu.CompilerParams(collective_id=0, has_side_effects=True, vmem_limit_bytes=24 * MIB),
        name="project",
    )(lengths, x, wq, wk, wv, wo, k_cache, v_cache)


def attend_kernel(len_ref, q_ref, kn_ref, vn_ref, os_ref, k_hbm, v_hbm, o_ref, kn_out, vn_out,
                  kl, vl, qf, knf, vnf, acc, lidx, lchunks, k_sem, v_sem, new_sem):
    me = lax.axis_index("model")
    base = me * LOCAL
    new_k = pltpu.make_async_copy(kn_ref, kn_out, new_sem.at[0])
    new_v = pltpu.make_async_copy(vn_ref, vn_out, new_sem.at[1])

    def each_part(i, slot, action):
        seq = base + lidx[i]
        chunks = lchunks[i]
        first = 0
        for size in (8, 4, 2, 1):
            rows = pl.ds(pl.multiple_of(first * CHUNK, CHUNK), size * CHUNK)

            @pl.when(chunks & size != 0)
            def _():
                for cache, dst, sem in ((k_hbm, kl, k_sem), (v_hbm, vl, v_sem)):
                    for half in range(2):
                        action(pltpu.make_async_copy(
                            cache.at[seq, 0, rows, pl.ds(half * HALFW, HALFW)],
                            dst.at[slot, half, rows, :], sem.at[slot]))

            first = first + (chunks & size)

    def fetch(i, slot, priority=1):
        each_part(i, slot, lambda copy: copy.start(priority=priority))

    def scan(i, count):
        length = len_ref[base + i]
        lidx[count] = i
        lchunks[count] = jnp.right_shift(length + (CHUNK - 1), CHUNK.bit_length() - 1)
        is_long = length > SHORT

        @pl.when(is_long & (count < 2))
        def _():
            fetch(count, count, 0)

        @pl.when(is_long & (count >= 2) & (count < AHEAD))
        def _():
            fetch(count, count)

        return count + jnp.where(is_long, 1, 0)

    n_long = lax.fori_loop(0, LOCAL, scan, jnp.int32(0))
    new_k.start()
    new_v.start()
    own = span(me, LOCAL)
    qf[...] = q_ref[...].astype(F32)
    knf[...] = kn_ref[own, :].astype(F32)
    vnf[...] = vn_ref[own, :].astype(F32)
    acc[...] = os_ref[...].astype(F32)

    def rows_of(ref, slot, rows):
        return jnp.concatenate([ref[slot, half, pl.ds(0, rows), :] for half in range(2)], axis=-1)

    def one_long(i, slot, rows):
        seq = lidx[i]
        at = pl.ds(seq, 1)
        q8 = jnp.concatenate([qf[h, at, :] for h in range(HEADS)], axis=0)
        s = lax.dot_general(q8.astype(BF), rows_of(kl, slot, rows), DIMS_T, preferred_element_type=F32) * SCALE
        s = jnp.where(lax.broadcasted_iota(jnp.int32, s.shape, 1) < len_ref[base + seq], s, -jnp.inf)
        s_new = jnp.sum(q8 * knf[at, :], axis=-1, keepdims=True) * SCALE
        e, e_new, total = softmax_parts(s, s_new)
        num = jnp.dot(e, rows_of(vl, slot, rows), preferred_element_type=F32)
        return seq, (num + e_new * vnf[at, :]) / total

    def wait_and_clear(i, slot, most):
        each_part(i, slot, lambda copy: copy.wait())

        @pl.loop(lchunks[i], most)
        def _(c):
            vl[slot, :, span(c, CHUNK), :] = jnp.zeros((2, CHUNK, HALFW), BF)

    def step(pair, slot):
        a = pair * 2
        alone = a + 1 >= n_long
        b = jnp.where(alone, a, a + 1)
        slot_b = jnp.where(alone, slot, slot + 1)
        most = jnp.maximum(lchunks[a], lchunks[b])
        wait_and_clear(a, slot, most)

        @pl.when(jnp.logical_not(alone))
        def _():
            wait_and_clear(b, slot + 1, most)

        later = jnp.where(slot >= SLOTS - AHEAD, slot + AHEAD - SLOTS, slot + AHEAD)
        for j in range(2):
            @pl.when(a + AHEAD + j < n_long)
            def _():
                fetch(a + AHEAD + j, later + j)

        for n in range(1, MAXLEN // CHUNK + 1):
            @pl.when(most == n)
            def _():
                results = [one_long(i, at, n * CHUNK) for i, at in ((a, slot), (b, slot_b))]
                for seq, out in results:
                    for h in range(HEADS):
                        acc[h, pl.ds(seq, 1), :] = out[h:h + 1, :]

        return jnp.where(slot + 2 >= SLOTS, 0, slot + 2)

    lax.fori_loop(0, jnp.right_shift(n_long + 1, 1), step, jnp.int32(0))
    o_ref[...] = acc[...].astype(BF)
    new_k.wait()
    new_v.wait()


def attend(lengths, q, k_new, v_new, o_short, k_cache, v_cache):
    rows = k_new.shape[0]
    any_spec = pl.BlockSpec(memory_space=pl.ANY)
    vmem_spec = pl.BlockSpec(memory_space=pltpu.VMEM)
    return pl.pallas_call(
        attend_kernel,
        out_shape=(
            jax.ShapeDtypeStruct((HEADS, LOCAL, HD), BF),
            jax.ShapeDtypeStruct((rows, HD), BF),
            jax.ShapeDtypeStruct((rows, HD), BF),
        ),
        in_specs=[pl.BlockSpec(memory_space=pltpu.SMEM)] + [vmem_spec] * 4 + [any_spec] * 2,
        out_specs=(vmem_spec, any_spec, any_spec),
        scratch_shapes=[
            pltpu.VMEM((SLOTS, 2, MAXLEN, HALFW), BF),
            pltpu.VMEM((SLOTS, 2, MAXLEN, HALFW), BF),
            pltpu.VMEM((HEADS, LOCAL, HD), F32),
            pltpu.VMEM((LOCAL, HD), F32),
            pltpu.VMEM((LOCAL, HD), F32),
            pltpu.VMEM((HEADS, LOCAL, HD), F32),
            pltpu.SMEM((LOCAL + 8,), jnp.int32),
            pltpu.SMEM((LOCAL + 8,), jnp.int32),
            pltpu.SemaphoreType.DMA((SLOTS,)),
            pltpu.SemaphoreType.DMA((SLOTS,)),
            pltpu.SemaphoreType.DMA((2,)),
        ],
        compiler_params=pltpu.CompilerParams(vmem_limit_bytes=24 * MIB),
        cost_estimate=pl.CostEstimate(flops=4 * 10 ** 9, bytes_accessed=10 ** 7, transcendentals=10 ** 6),
        name="attend",
    )(lengths, q, k_new, v_new, o_short, k_cache, v_cache)


HALF = HEADS // 2
X, Y, D, S = 2, 4, 6, 1
MSGS = 11


def output_kernel(o_ref, wo_hbm, wx_ref, wy_ref, wd_ref, x_hbm, y_ref, og, wc, xc, load_sem, wss, wrs, os, orr, ys, yr):
    me, _, _, _ = coords()
    chip = me // 2
    load_x = pltpu.make_async_copy(x_hbm.at[:, span(chip, 2 * HD)], xc, load_sem.at[0])
    load_x.start()
    w_loads, w_copies, w_recvs = [], [], []
    for i, (rel, ref) in enumerate(((0, wo_hbm.at[:, span(chip, 2 * HD)]), (D, wd_ref), (X, wx_ref), (Y, wy_ref))):
        w_loads.append(pltpu.make_async_copy(ref, wc.at[peer(rel)], load_sem.at[1 + i]))
        w_loads[-1].start()
        w_copies.append(remote(ref, wc.at[peer(rel)], wss.at[i], wrs.at[i], S))
        w_recvs.append(remote(ref, wc.at[peer(rel + S)], wss.at[i], wrs.at[i], S))
    entry_barrier((X, Y, S))
    started = []

    def go(copy):
        copy.start()
        started.append(copy)

    def o_copy(owner_rel, half, to, index):
        part = pl.ds(half * HALF, HALF)
        dst = og.at[peer(owner_rel) // 2, part]
        return remote(o_ref.at[part] if owner_rel == 0 else dst, dst, os.at[index], orr.at[index], to)

    def y_copy(col_rel, row_rel, half, to, index):
        if half is None:
            rows = span(peer(row_rel), LOCAL)
        else:
            rows = span(peer(row_rel) * 2 + half, LOCAL // 2)
        ref = y_ref.at[rows, span(peer(col_rel) // 2, 2 * HD)]
        return remote(ref, ref, ys.at[index], yr.at[index], to)

    def compute(step, rel):
        total = jnp.zeros((LOCAL, 2 * HD), F32)
        for h in range(HEADS):
            total = total + jnp.dot(og[peer(rel) // 2, h], wc[h], preferred_element_type=F32)
        rows = span(peer(rel), LOCAL)
        y_ref[rows, span(chip, 2 * HD)] = (xc[rows, :].astype(F32) + total).astype(BF)
        b = step * MSGS
        go(y_copy(0, rel, 0, X, b + 0))
        go(y_copy(0, rel, 1, Y, b + 1))
        go(y_copy(0, rel, 1, X, b + 2))
        go(y_copy(0, rel, 0, Y, b + 3))
        go(y_copy(0, rel, None, S, b + 4))

    go(o_copy(0, 0, X, 0))
    go(o_copy(0, 1, Y, 1))
    go(o_copy(0, 1, X, 2))
    go(o_copy(0, 0, Y, 3))
    for c in w_copies:
        go(c)
    og[chip] = o_ref[...]
    load_x.wait()
    for load in w_loads:
        load.wait()
    for c in w_recvs:
        c.wait_recv()
    compute(0, 0)
    o_copy(X, 0, X, 0).wait_recv()
    go(o_copy(X, 0, Y, 4))
    o_copy(Y, 1, Y, 1).wait_recv()
    go(o_copy(Y, 1, X, 5))
    o_copy(X, 1, X, 2).wait_recv()
    compute(1, X)
    o_copy(Y, 0, Y, 3).wait_recv()
    compute(2, Y)
    o_copy(D, 0, Y, 4).wait_recv()
    o_copy(D, 1, X, 5).wait_recv()
    compute(3, D)

    def xor(a, b):
        return ((a // 4 + b // 4) % 2) * 4 + ((a // 2 + b // 2) % 2) * 2 + (a + b) % 2

    order = (0, X, Y, D)
    for step, rel in enumerate(order):
        b = step * MSGS
        at_x, at_y = xor(rel, X), xor(rel, Y)
        y_copy(X, at_x, 0, X, b + 0).wait_recv()
        go(y_copy(X, at_x, 0, Y, b + 5))
        y_copy(Y, at_y, 1, Y, b + 1).wait_recv()
        go(y_copy(Y, at_y, 1, X, b + 6))
        y_copy(X, at_x, 1, X, b + 2).wait_recv()
        go(y_copy(X, at_x, None, S, b + 7))
        y_copy(Y, at_y, 0, Y, b + 3).wait_recv()
        go(y_copy(Y, at_y, None, S, b + 8))
    for step, rel in enumerate(order):
        b = step * MSGS
        at_d = xor(rel, D)
        y_copy(D, at_d, 0, Y, b + 5).wait_recv()
        go(y_copy(D, at_d, 0, S, b + 9))
        y_copy(D, at_d, 1, X, b + 6).wait_recv()
        go(y_copy(D, at_d, 1, S, b + 10))
    for step, rel in enumerate(order):
        b = step * MSGS
        y_copy(S, rel + S, None, S, b + 4).wait_recv()
        y_copy(X + S, xor(rel, X) + S, None, S, b + 7).wait_recv()
        y_copy(Y + S, xor(rel, Y) + S, None, S, b + 8).wait_recv()
        y_copy(D + S, xor(rel, D) + S, 0, S, b + 9).wait_recv()
        y_copy(D + S, xor(rel, D) + S, 1, S, b + 10).wait_recv()
    for copy in started:
        copy.wait_send()


def output(o, wo, wx, wy, wd, x):
    rows, width = x.shape
    hbm_spec = pl.BlockSpec(memory_space=pltpu.HBM)
    vmem_spec = pl.BlockSpec(memory_space=pltpu.VMEM)
    return pl.pallas_call(
        output_kernel,
        out_shape=jax.ShapeDtypeStruct((rows, width), BF),
        in_specs=[vmem_spec, hbm_spec, vmem_spec, vmem_spec, hbm_spec, hbm_spec],
        out_specs=vmem_spec,
        scratch_shapes=[
            pltpu.VMEM((4, HEADS, LOCAL, HD), BF),
            pltpu.VMEM((HEADS, HD, 2 * HD), BF),
            pltpu.VMEM((rows, 2 * HD), BF),
            pltpu.SemaphoreType.DMA((5,)),
            pltpu.SemaphoreType.DMA((4,)),
            pltpu.SemaphoreType.DMA((4,)),
            pltpu.SemaphoreType.DMA((6,)),
            pltpu.SemaphoreType.DMA((6,)),
            pltpu.SemaphoreType.DMA((4 * MSGS,)),
            pltpu.SemaphoreType.DMA((4 * MSGS,)),
        ],
        compiler_params=pltpu.CompilerParams(collective_id=1, has_side_effects=True, vmem_limit_bytes=24 * MIB),
        name="output",
    )(o, wo, wx, wy, wd, x)


def solution(mesh):
    def local_step(x, w_query, w_key, w_value, w_out, k_cache, v_cache, lengths):
        x, w_query, w_key, w_value, w_out = (
            pltpu.with_memory_space_constraint(a, pltpu.HBM) for a in (x, w_query, w_key, w_value, w_out))
        pinned = pltpu.with_memory_space_constraint(lengths, pltpu.HBM)
        q, k_new, v_new, wx, wy, o_short, wd = project(pinned, x, w_query, w_key, w_value, w_out, k_cache, v_cache)
        wd = lax.ppermute(wd, "model", [(d, d ^ D) for d in range(8)])
        o, k_new, v_new = attend(lengths, q, k_new, v_new, o_short, k_cache, v_cache)
        y = output(o, w_out, wx, wy, wd, x)
        return y, k_new[:, None, :], v_new[:, None, :]

    rows_spec = P("replica")
    return jax.shard_map(
        local_step,
        mesh=mesh,
        in_specs=(P("replica", None), P(None, "model"), P(), P(), P("model", None), rows_spec, rows_spec, rows_spec),
        out_specs=(rows_spec, rows_spec, rows_spec),
        check_vma=False,
    )
```

profile of v0, /device:TPU:0, one launch (start us, length us, event | category | flops | bytes accessed | tf_op | source)
XLA Modules:
  0.0 48.8 jit_solution(13991386051634232646)
XLA Ops:
  0.6 0.0 copy-start
  0.6 15.5 %project.1 = (bf16[8,64,256]{2,1,0:T(8,128)(2,1)S(1)}, bf16[512,256]{1,0:T(8,128)(2,1)S(1)}, bf16[512,256]{1,0:T(8,128)(2,1)S(1)}, bf16[256,512]{1,0:T(8,128)(2,...) custom-call(s32[512]{0:T(512)} %len_ref.1, ...), custom_call_target="tpu_custom_call" | custom-call | tf_op jit(solution)/shard_map/project/pallas_call | solution.py:150
  16.1 1.8 %collective-permute-start = (bf16[256,512]{1,0:T(8,128)(2,1)}, bf16[256,512]{1,0:T(8,128)(2,1)}, u32[]{:S(2)}, u32[]{:S(2)}) collective-permute-start(bf16[256,512]{1,0:T(8,128)(2,1)} %get-tuple-element.20), channel_id=1, source_target_pairs={{0,6},{1,7},{2,4},{3,5},{4,2},{5,3},{6,0},{7,1}} | collective-permute-start | bytes 786440 | tf_op jit(solution)/shard_map/ppermute | solution.py:464
  17.9 0.0 copy-done
  17.9 4.9 %attend.1 = (bf16[8,64,256]{2,1,0:T(8,128)(2,1)S(1)}, bf16[512,256]{1,0:T(8,128)(2,1)}, bf16[512,256]{1,0:T(8,128)(2,1)}) custom-call(s32[512]{0:T(512)S(1)} %copy-done, bf16[8,64,256]{2,1,0:T(8,128)(2,1)S(1)} %get-tuple-element.13.q_ref, bf16[512,256]{1,0:T(8,128)(2,1)S(1)} %get-tuple-element.14.kn_ref, bf16[512,256]{1,0:T(8,128)(2,1)S(1)} %get-tuple-element.15.vn_ref, ...), custom_call_target="tpu_custom_call" | custom-call | flops 4000000000 | bytes 10000000 | tf_op jit(solution)/shard_map/attend/pallas_call | solution.py:297
  22.8 2.7 %collective-permute-done.wd_ref = bf16[256,512]{1,0:T(8,128)(2,1)} collective-permute-done((bf16[256,512]{1,0:T(8,128)(2,1)}, bf16[256,512]{1,0:T(8,128)(2,1)}, u32[]{:S(2)}, u32[]{:S(2)}) %collective-permute-start) | collective-permute-done | bytes 262176 | tf_op jit(solution)/shard_map/ppermute | solution.py:464
  25.4 22.1 %output.1 = bf16[512,2048]{1,0:T(8,128)(2,1)S(1)} custom-call(bf16[8,64,256]{2,1,0:T(8,128)(2,1)S(1)} %get-tuple-element.17.o_ref, bf16[256,2048]{1,0:T(8,128)(2,1)} %wo_hbm.3, bf16[256,512]{1,0:T(8,128)(2,1)S(1)} %get-tuple-element.18.wx_ref, bf16[256,512]{1,0:T(8,128)(2,1)S(1)} %get-tuple-element.19.wy_ref, bf16[256,512]{1,0:T(8,128)(2,1)} %collective-permute-done.wd_ref, ...), custom_call_target="tpu_custom_call" | custom-call | tf_op jit(solution)/shard_map/output/pallas_call | solution.py:436
  47.5 1.3 %copy.12 = bf16[512,2048]{1,0:T(8,128)(2,1)} copy(bf16[512,2048]{1,0:T(8,128)(2,1)S(1)} %output.1) | data formatting | bytes 4194304
Async XLA Ops:
  0.6 17.3 %copy-start = (s32[512]{0:T(512)S(1)}, s32[512]{0:T(512)}, u32[]{:S(2)}) copy-start(s32[512]{0:T(512)} %len_ref.1) | copy-start | bytes 6148
  16.1 9.3 %collective-permute-start = (bf16[256,512]{1,0:T(8,128)(2,1)}, bf16[256,512]{1,0:T(8,128)(2,1)}, u32[]{:S(2)}, u32[]{:S(2)}) collective-permute-start(bf16[256,512]{1,0:T(8,128)(2,1)} %get-tuple-element.20), channel_id=1, source_target_pairs={{0,6},{1,7},{2,4},{3,5},{4,2},{5,3},{6,0},{7,1}} | collective-permute-start | bytes 786440 | tf_op jit(solution)/shard_map/ppermute | solution.py:464
where the time goes:
time: 49.1 us; the launch traced here: 48.8 us
  Pallas kernels  42.4 us (86%)
  waiting for transfers between devices  2.67 us (5%)
  starting transfers between devices  1.77 us (4%)
  local copies, waits for them, and re-layouts  1.33 us (3%)
  between operations  0.66 us (1%)
    pallas_call x1, Pallas kernels, output(): pl.pallas_call(output_kernel, out_shape=jax.ShapeDtypeStruct((rows, width...  22.1 us
    pallas_call x1, Pallas kernels, project(): pl.pallas_call(project_kernel, out_shape=(jax.ShapeDtypeStruct((HEADS, LO...  15.5 us
    pallas_call x1, Pallas kernels, attend(): pl.pallas_call(attend_kernel, out_shape=(jax.ShapeDtypeStruct((HEADS, LOC...  4.85 us
    ppermute x1, waiting for transfers between devices, local_step(): wd = lax.ppermute(wd, 'model', [(d, d ^ D) for d in range(8)])  2.67 us
    ppermute x1, starting transfers between devices, local_step(): wd = lax.ppermute(wd, 'model', [(d, d ^ D) for d in range(8)])  1.77 us
    unnamed x3, local copies, waits for them, and re-layouts  1.33 us
  transfers between devices with their start and end apart: 1, of which 1 were waited for; matrix products, arithmetic and copies ran while one was open for 0% of the time, Pallas kernels for 10%

commit v1 on v0

--- a/solution.py
+++ b/solution.py
@@ -14,7 +14,7 @@
 GROUP = 16
 CHUNK = 256
 MAXLEN = 2048
-SLOTS = 6
+SLOTS = 8
 AHEAD = 4
 HALFW = 128
 MIB = 2 ** 20
@@ -184,13 +184,13 @@
 
 
 def attend_kernel(len_ref, q_ref, kn_ref, vn_ref, os_ref, k_hbm, v_hbm, o_ref, kn_out, vn_out,
-                  kl, vl, qf, knf, vnf, acc, lidx, lchunks, k_sem, v_sem, new_sem):
+                  kl, vl, qf, knf, vnf, acc, es, st, lidx, lchunks, k_sem, v_sem, new_sem):
     me = lax.axis_index("model")
     base = me * LOCAL
     new_k = pltpu.make_async_copy(kn_ref, kn_out, new_sem.at[0])
     new_v = pltpu.make_async_copy(vn_ref, vn_out, new_sem.at[1])
 
-    def each_part(i, slot, action):
+    def each_part(i, slot, cache, dst, sem, action):
         seq = base + lidx[i]
         chunks = lchunks[i]
         first = 0
@@ -199,16 +199,20 @@
 
             @pl.when(chunks & size != 0)
             def _():
-                for cache, dst, sem in ((k_hbm, kl, k_sem), (v_hbm, vl, v_sem)):
-                    for half in range(2):
-                        action(pltpu.make_async_copy(
-                            cache.at[seq, 0, rows, pl.ds(half * HALFW, HALFW)],
-                            dst.at[slot, half, rows, :], sem.at[slot]))
+                for half in range(2):
+                    action(pltpu.make_async_copy(
+                        cache.at[seq, 0, rows, pl.ds(half * HALFW, HALFW)],
+                        dst.at[slot, half, rows, :], sem.at[slot]))
 
             first = first + (chunks & size)
 
-    def fetch(i, slot, priority=1):
-        each_part(i, slot, lambda copy: copy.start(priority=priority))
+    def start(copy):
+        copy.start()
+
+    def wait(copy):
+        copy.wait()
+
+    keys, values = (k_hbm, kl, k_sem), (v_hbm, vl, v_sem)
 
     def scan(i, count):
         length = len_ref[base + i]
@@ -216,17 +220,22 @@
         lchunks[count] = jnp.right_shift(length + (CHUNK - 1), CHUNK.bit_length() - 1)
         is_long = length > SHORT
 
-        @pl.when(is_long & (count < 2))
+        @pl.when(is_long & (count < AHEAD))
         def _():
-            fetch(count, count, 0)
-
-        @pl.when(is_long & (count >= 2) & (count < AHEAD))
-        def _():
-            fetch(count, count)
+            each_part(count, count, *keys, start)
 
         return count + jnp.where(is_long, 1, 0)
 
     n_long = lax.fori_loop(0, LOCAL, scan, jnp.int32(0))
+
+    @pl.loop(0, SLOTS * 2)
+    def _(i):
+        vl[jnp.right_shift(i, 1), i & 1] = jnp.zeros((MAXLEN, HALFW), BF)
+
+    @pl.loop(0, jnp.minimum(n_long, AHEAD))
+    def _(i):
+        each_part(i, i, *values, start)
+
     new_k.start()
     new_v.start()
     own = span(me, LOCAL)
@@ -238,53 +247,85 @@
     def rows_of(ref, slot, rows):
         return jnp.concatenate([ref[slot, half, pl.ds(0, rows), :] for half in range(2)], axis=-1)
 
-    def one_long(i, slot, rows):
-        seq = lidx[i]
-        at = pl.ds(seq, 1)
+    def score(i, slot, n):
+        rows = n * CHUNK
+        at = pl.ds(lidx[i], 1)
         q8 = jnp.concatenate([qf[h, at, :] for h in range(HEADS)], axis=0)
         s = lax.dot_general(q8.astype(BF), rows_of(kl, slot, rows), DIMS_T, preferred_element_type=F32) * SCALE
-        s = jnp.where(lax.broadcasted_iota(jnp.int32, s.shape, 1) < len_ref[base + seq], s, -jnp.inf)
+        s = jnp.where(lax.broadcasted_iota(jnp.int32, s.shape, 1) < len_ref[base + lidx[i]], s, -jnp.inf)
         s_new = jnp.sum(q8 * knf[at, :], axis=-1, keepdims=True) * SCALE
-        e, e_new, total = softmax_parts(s, s_new)
-        num = jnp.dot(e, rows_of(vl, slot, rows), preferred_element_type=F32)
-        return seq, (num + e_new * vnf[at, :]) / total
-
-    def wait_and_clear(i, slot, most):
-        each_part(i, slot, lambda copy: copy.wait())
-
-        @pl.loop(lchunks[i], most)
-        def _(c):
-            vl[slot, :, span(c, CHUNK), :] = jnp.zeros((2, CHUNK, HALFW), BF)
-
-    def step(pair, slot):
-        a = pair * 2
+        return softmax_parts(s, s_new)
+
+    def weigh(i, slot, j, n):
+        num = jnp.dot(es[j, :, pl.ds(0, n * CHUNK)], rows_of(vl, slot, n * CHUNK), preferred_element_type=F32)
+        return (num + st[j, 0, :, 0:1] * vnf[pl.ds(lidx[i], 1), :]) / st[j, 1, :, 0:1]
+
+    def work(now, before, n):
+        outs = [weigh(i, slot, j, n) for j, (i, slot) in enumerate(before)]
+        parts = [score(i, slot, n) for i, slot in now]
+        for (i, _), out in zip(before, outs):
+            for h in range(HEADS):
+                acc[h, pl.ds(lidx[i], 1), :] = out[h:h + 1, :]
+        for j, (e, e_new, total) in enumerate(parts):
+            es[j, :, pl.ds(0, n * CHUNK)] = e
+            if n * CHUNK < MAXLEN:
+                es[j, :, pl.ds(n * CHUNK, MAXLEN - n * CHUNK)] = jnp.zeros((HEADS, MAXLEN - n * CHUNK), BF)
+            st[j, 0] = jnp.broadcast_to(e_new, (HEADS, 128))
+            st[j, 1] = jnp.broadcast_to(total, (HEADS, 128))
+
+    pairs = jnp.right_shift(n_long + 1, 1)
+
+    def members(p):
+        a = p * 2
+        slot = a & (SLOTS - 1)
         alone = a + 1 >= n_long
-        b = jnp.where(alone, a, a + 1)
-        slot_b = jnp.where(alone, slot, slot + 1)
-        most = jnp.maximum(lchunks[a], lchunks[b])
-        wait_and_clear(a, slot, most)
-
-        @pl.when(jnp.logical_not(alone))
+        return a, slot, jnp.where(alone, a, a + 1), jnp.where(alone, slot, slot + 1), alone
+
+    @pl.loop(0, jnp.where(n_long > 0, pairs + 1, 0))
+    def _(p):
+        a, slot_a, b, slot_b, alone = members(jnp.minimum(p, pairs - 1))
+        c, slot_c, d, slot_d, alone_before = members(jnp.maximum(p - 1, 0))
+        has_now, has_before = p < pairs, p > 0
+
+        @pl.when(has_now)
         def _():
-            wait_and_clear(b, slot + 1, most)
-
-        later = jnp.where(slot >= SLOTS - AHEAD, slot + AHEAD - SLOTS, slot + AHEAD)
+            each_part(a, slot_a, *keys, wait)
+
+        @pl.when(has_now & jnp.logical_not(alone))
+        def _():
+            each_part(b, slot_b, *keys, wait)
+
+        @pl.when(has_before)
+        def _():
+            each_part(c, slot_c, *values, wait)
+
+        @pl.when(has_before & jnp.logical_not(alone_before))
+        def _():
+            each_part(d, slot_d, *values, wait)
+
         for j in range(2):
-            @pl.when(a + AHEAD + j < n_long)
+            i = p * 2 + AHEAD + j
+
+            @pl.when(i < n_long)
             def _():
-                fetch(a + AHEAD + j, later + j)
-
-        for n in range(1, MAXLEN // CHUNK + 1):
-            @pl.when(most == n)
+                each_part(i, i & (SLOTS - 1), *keys, start)
+                each_part(i, i & (SLOTS - 1), *values, start)
+
+        now, before = ((a, slot_a), (b, slot_b)), ((c, slot_c), (d, slot_d))
+        most_now = jnp.maximum(lchunks[a], lchunks[b])
+        most_before = jnp.maximum(lchunks[c], lchunks[d])
+        for cond, most, args in (
+            (has_now & has_before, jnp.maximum(most_now, most_before), (now, before)),
+            (p == 0, most_now, (now, ())),
+            (p == pairs, most_before, ((), before)),
+        ):
+            @pl.when(cond)
             def _():
-                results = [one_long(i, at, n * CHUNK) for i, at in ((a, slot), (b, slot_b))]
-                for seq, out in results:
-                    for h in range(HEADS):
-                        acc[h, pl.ds(seq, 1), :] = out[h:h + 1, :]
-
-        return jnp.where(slot + 2 >= SLOTS, 0, slot + 2)
-
-    lax.fori_loop(0, jnp.right_shift(n_long + 1, 1), step, jnp.int32(0))
+                for n in range(1, MAXLEN // CHUNK + 1):
+                    @pl.when(most == n)
+                    def _():
+                        work(*args, n)
+
     o_ref[...] = acc[...].astype(BF)
     new_k.wait()
     new_v.wait()
@@ -310,6 +351,8 @@
             pltpu.VMEM((LOCAL, HD), F32),
             pltpu.VMEM((LOCAL, HD), F32),
             pltpu.VMEM((HEADS, LOCAL, HD), F32),
+            pltpu.VMEM((2, HEADS, MAXLEN), BF),
+            pltpu.VMEM((2, 2, HEADS, 128), F32),
             pltpu.SMEM((LOCAL + 8,), jnp.int32),
             pltpu.SMEM((LOCAL + 8,), jnp.int32),
             pltpu.SemaphoreType.DMA((SLOTS,)),

time: 49.1 us -> 49.9 us (1.016)
  Pallas kernels: 42.4 us -> 45.3 us
  waiting for transfers between devices: 2.67 us -> 0.35 us
    pallas_call x1, Pallas kernels: 4.85 us -> 7.17 us  [attend(): pl.pallas_call(attend_kernel, out_shape=(jax.ShapeDtypeStruct((HEADS, LOC...]
    ppermute x1, waiting for transfers between devices: 2.67 us -> 0.35 us  [local_step(): wd = lax.ppermute(wd, 'model', [(d, d ^ D) for d in range(8)])]
    pallas_call x1, Pallas kernels: 22.1 us -> 22.7 us  [output(): pl.pallas_call(output_kernel, out_shape=jax.ShapeDtypeStruct((rows, width...]
  transfers between devices with their start and end apart: 1 -> 1, of which waited for: 1 -> 1; matrix products, arithmetic and copies ran while one was open for 0% -> 0% of each run, Pallas kernels for 10% -> 15%
where the time goes in v1:
time: 49.9 us; the launch traced here: 49.4 us
  Pallas kernels  45.3 us (91%)
  starting transfers between devices  1.77 us (4%)
  local copies, waits for them, and re-layouts  1.33 us (3%)
  between operations  0.66 us (1%)
    pallas_call x1, Pallas kernels, output(): pl.pallas_call(output_kernel, out_shape=jax.ShapeDtypeStruct((rows, width...  22.7 us
    pallas_call x1, Pallas kernels, project(): pl.pallas_call(project_kernel, out_shape=(jax.ShapeDtypeStruct((HEADS, LO...  15.5 us
    pallas_call x1, Pallas kernels, attend(): pl.pallas_call(attend_kernel, out_shape=(jax.ShapeDtypeStruct((HEADS, LOC...  7.17 us
    ppermute x1, starting transfers between devices, local_step(): wd = lax.ppermute(wd, 'model', [(d, d ^ D) for d in range(8)])  1.77 us
    unnamed x3, local copies, waits for them, and re-layouts  1.33 us
  transfers between devices with their start and end apart: 1, of which 1 were waited for; matrix products, arithmetic and copies ran while one was open for 0% of the time, Pallas kernels for 15%

profile of v1, /device:TPU:0, one launch (start us, length us, event | category | flops | bytes accessed | tf_op | source)
XLA Modules:
  0.0 49.4 jit_solution(4319883738355304586)
XLA Ops:
  0.6 0.0 copy-start
  0.6 15.5 %project.1 = (bf16[8,64,256]{2,1,0:T(8,128)(2,1)S(1)}, bf16[512,256]{1,0:T(8,128)(2,1)S(1)}, bf16[512,256]{1,0:T(8,128)(2,1)S(1)}, bf16[256,512]{1,0:T(8,128)(2,...) custom-call(s32[512]{0:T(512)} %len_ref.1, ...), custom_call_target="tpu_custom_call" | custom-call | tf_op jit(solution)/shard_map/project/pallas_call | solution.py:150
  16.1 1.8 %collective-permute-start = (bf16[256,512]{1,0:T(8,128)(2,1)}, bf16[256,512]{1,0:T(8,128)(2,1)}, u32[]{:S(2)}, u32[]{:S(2)}) collective-permute-start(bf16[256,512]{1,0:T(8,128)(2,1)} %get-tuple-element.20), channel_id=1, source_target_pairs={{0,6},{1,7},{2,4},{3,5},{4,2},{5,3},{6,0},{7,1}} | collective-permute-start | bytes 786440 | tf_op jit(solution)/shard_map/ppermute | solution.py:507
  17.9 0.0 copy-done
  17.9 7.2 %attend.1 = (bf16[8,64,256]{2,1,0:T(8,128)(2,1)S(1)}, bf16[512,256]{1,0:T(8,128)(2,1)}, bf16[512,256]{1,0:T(8,128)(2,1)}) custom-call(s32[512]{0:T(512)S(1)} %copy-done, bf16[8,64,256]{2,1,0:T(8,128)(2,1)S(1)} %get-tuple-element.13.q_ref, bf16[512,256]{1,0:T(8,128)(2,1)S(1)} %get-tuple-element.14.kn_ref, bf16[512,256]{1,0:T(8,128)(2,1)S(1)} %get-tuple-element.15.vn_ref, ...), custom_call_target="tpu_custom_call" | custom-call | flops 4000000000 | bytes 10000000 | tf_op jit(solution)/shard_map/attend/pallas_call | solution.py:338
  25.1 0.3 collective-permute-done.wd_ref
  25.4 22.7 %output.1 = bf16[512,2048]{1,0:T(8,128)(2,1)S(1)} custom-call(bf16[8,64,256]{2,1,0:T(8,128)(2,1)S(1)} %get-tuple-element.17.o_ref, bf16[256,2048]{1,0:T(8,128)(2,1)} %wo_hbm.3, bf16[256,512]{1,0:T(8,128)(2,1)S(1)} %get-tuple-element.18.wx_ref, bf16[256,512]{1,0:T(8,128)(2,1)S(1)} %get-tuple-element.19.wy_ref, bf16[256,512]{1,0:T(8,128)(2,1)} %collective-permute-done.wd_ref, ...), custom_call_target="tpu_custom_call" | custom-call | tf_op jit(solution)/shard_map/output/pallas_call | solution.py:479
  48.1 1.3 %copy.12 = bf16[512,2048]{1,0:T(8,128)(2,1)} copy(bf16[512,2048]{1,0:T(8,128)(2,1)S(1)} %output.1) | data formatting | bytes 4194304
Async XLA Ops:
  0.6 17.3 %copy-start = (s32[512]{0:T(512)S(1)}, s32[512]{0:T(512)}, u32[]{:S(2)}) copy-start(s32[512]{0:T(512)} %len_ref.1) | copy-start | bytes 6148
  16.1 9.3 %collective-permute-start = (bf16[256,512]{1,0:T(8,128)(2,1)}, bf16[256,512]{1,0:T(8,128)(2,1)}, u32[]{:S(2)}, u32[]{:S(2)}) collective-permute-start(bf16[256,512]{1,0:T(8,128)(2,1)} %get-tuple-element.20), channel_id=1, source_target_pairs={{0,6},{1,7},{2,4},{3,5},{4,2},{5,3},{6,0},{7,1}} | collective-permute-start | bytes 786440 | tf_op jit(solution)/shard_map/ppermute | solution.py:507

commit v2 on v0

--- a/solution.py
+++ b/solution.py
@@ -199,16 +199,16 @@
 
             @pl.when(chunks & size != 0)
             def _():
-                for cache, dst, sem in ((k_hbm, kl, k_sem), (v_hbm, vl, v_sem)):
+                for queue, (cache, dst, sem) in enumerate(((k_hbm, kl, k_sem), (v_hbm, vl, v_sem))):
                     for half in range(2):
                         action(pltpu.make_async_copy(
                             cache.at[seq, 0, rows, pl.ds(half * HALFW, HALFW)],
-                            dst.at[slot, half, rows, :], sem.at[slot]))
+                            dst.at[slot, half, rows, :], sem.at[slot]), queue)
 
             first = first + (chunks & size)
 
-    def fetch(i, slot, priority=1):
-        each_part(i, slot, lambda copy: copy.start(priority=priority))
+    def fetch(i, slot):
+        each_part(i, slot, lambda copy, queue: copy.start(priority=queue))
 
     def scan(i, count):
         length = len_ref[base + i]
@@ -216,11 +216,7 @@
         lchunks[count] = jnp.right_shift(length + (CHUNK - 1), CHUNK.bit_length() - 1)
         is_long = length > SHORT
 
-        @pl.when(is_long & (count < 2))
-        def _():
-            fetch(count, count, 0)
-
-        @pl.when(is_long & (count >= 2) & (count < AHEAD))
+        @pl.when(is_long & (count < AHEAD))
         def _():
             fetch(count, count)
 
@@ -250,7 +246,7 @@
         return seq, (num + e_new * vnf[at, :]) / total
 
     def wait_and_clear(i, slot, most):
-        each_part(i, slot, lambda copy: copy.wait())
+        each_part(i, slot, lambda copy, _: copy.wait())
 
         @pl.loop(lchunks[i], most)
         def _(c):

time: 49.1 us -> 49.3 us (level)
  Pallas kernels: 42.4 us -> 45 us
  waiting for transfers between devices: 2.67 us -> 0.19 us
    ppermute x1, waiting for transfers between devices: 2.67 us -> 0.19 us  [local_step(): wd = lax.ppermute(wd, 'model', [(d, d ^ D) for d in range(8)])]
    pallas_call x1, Pallas kernels: 4.85 us -> 7.33 us  [attend(): pl.pallas_call(attend_kernel, out_shape=(jax.ShapeDtypeStruct((HEADS, LOC...]
  transfers between devices with their start and end apart: 1 -> 1, of which waited for: 1 -> 1; matrix products, arithmetic and copies ran while one was open for 0% -> 0% of each run, Pallas kernels for 10% -> 15%
where the time goes in v2:
time: 49.3 us; the launch traced here: 49 us
  Pallas kernels  45 us (91%)
  starting transfers between devices  1.77 us (4%)
  local copies, waits for them, and re-layouts  1.33 us (3%)
  between operations  0.66 us (1%)
    pallas_call x1, Pallas kernels, output(): pl.pallas_call(output_kernel, out_shape=jax.ShapeDtypeStruct((rows, width...  22.2 us
    pallas_call x1, Pallas kernels, project(): pl.pallas_call(project_kernel, out_shape=(jax.ShapeDtypeStruct((HEADS, LO...  15.5 us
    pallas_call x1, Pallas kernels, attend(): pl.pallas_call(attend_kernel, out_shape=(jax.ShapeDtypeStruct((HEADS, LOC...  7.33 us
    ppermute x1, starting transfers between devices, local_step(): wd = lax.ppermute(wd, 'model', [(d, d ^ D) for d in range(8)])  1.77 us
    unnamed x3, local copies, waits for them, and re-layouts  1.33 us
  transfers between devices with their start and end apart: 1, of which 1 were waited for; matrix products, arithmetic and copies ran while one was open for 0% of the time, Pallas kernels for 15%

profile of v2, /device:TPU:0, one launch (start us, length us, event | category | flops | bytes accessed | tf_op | source)
XLA Modules:
  0.0 49.0 jit_solution(13007674328323357716)
XLA Ops:
  0.6 0.0 copy-start
  0.6 15.5 %project.1 = (bf16[8,64,256]{2,1,0:T(8,128)(2,1)S(1)}, bf16[512,256]{1,0:T(8,128)(2,1)S(1)}, bf16[512,256]{1,0:T(8,128)(2,1)S(1)}, bf16[256,512]{1,0:T(8,128)(2,...) custom-call(s32[512]{0:T(512)} %len_ref.1, ...), custom_call_target="tpu_custom_call" | custom-call | tf_op jit(solution)/shard_map/project/pallas_call | solution.py:150
  16.1 1.8 %collective-permute-start = (bf16[256,512]{1,0:T(8,128)(2,1)}, bf16[256,512]{1,0:T(8,128)(2,1)}, u32[]{:S(2)}, u32[]{:S(2)}) collective-permute-start(bf16[256,512]{1,0:T(8,128)(2,1)} %get-tuple-element.20), channel_id=1, source_target_pairs={{0,6},{1,7},{2,4},{3,5},{4,2},{5,3},{6,0},{7,1}} | collective-permute-start | bytes 786440 | tf_op jit(solution)/shard_map/ppermute | solution.py:460
  17.9 0.0 copy-done
  17.9 7.3 %attend.1 = (bf16[8,64,256]{2,1,0:T(8,128)(2,1)S(1)}, bf16[512,256]{1,0:T(8,128)(2,1)}, bf16[512,256]{1,0:T(8,128)(2,1)}) custom-call(s32[512]{0:T(512)S(1)} %copy-done, bf16[8,64,256]{2,1,0:T(8,128)(2,1)S(1)} %get-tuple-element.13.q_ref, bf16[512,256]{1,0:T(8,128)(2,1)S(1)} %get-tuple-element.14.kn_ref, bf16[512,256]{1,0:T(8,128)(2,1)S(1)} %get-tuple-element.15.vn_ref, ...), custom_call_target="tpu_custom_call" | custom-call | flops 4000000000 | bytes 10000000 | tf_op jit(solution)/shard_map/attend/pallas_call | solution.py:293
  25.2 0.2 collective-permute-done.wd_ref
  25.4 22.2 %output.1 = bf16[512,2048]{1,0:T(8,128)(2,1)S(1)} custom-call(bf16[8,64,256]{2,1,0:T(8,128)(2,1)S(1)} %get-tuple-element.17.o_ref, bf16[256,2048]{1,0:T(8,128)(2,1)} %wo_hbm.3, bf16[256,512]{1,0:T(8,128)(2,1)S(1)} %get-tuple-element.18.wx_ref, bf16[256,512]{1,0:T(8,128)(2,1)S(1)} %get-tuple-element.19.wy_ref, bf16[256,512]{1,0:T(8,128)(2,1)} %collective-permute-done.wd_ref, ...), custom_call_target="tpu_custom_call" | custom-call | tf_op jit(solution)/shard_map/output/pallas_call | solution.py:432
  47.6 1.3 %copy.12 = bf16[512,2048]{1,0:T(8,128)(2,1)} copy(bf16[512,2048]{1,0:T(8,128)(2,1)S(1)} %output.1) | data formatting | bytes 4194304
Async XLA Ops:
  0.6 17.3 %copy-start = (s32[512]{0:T(512)S(1)}, s32[512]{0:T(512)}, u32[]{:S(2)}) copy-start(s32[512]{0:T(512)} %len_ref.1) | copy-start | bytes 6148
  16.1 9.3 %collective-permute-start = (bf16[256,512]{1,0:T(8,128)(2,1)}, bf16[256,512]{1,0:T(8,128)(2,1)}, u32[]{:S(2)}, u32[]{:S(2)}) collective-permute-start(bf16[256,512]{1,0:T(8,128)(2,1)} %get-tuple-element.20), channel_id=1, source_target_pairs={{0,6},{1,7},{2,4},{3,5},{4,2},{5,3},{6,0},{7,1}} | collective-permute-start | bytes 786440 | tf_op jit(solution)/shard_map/ppermute | solution.py:460
